TPU v7x, 32 devices: a whole 2x2x4 slice. The times are simulated.
32 devices in a mesh: root: 4 (over z), virt: 4 (over y, x), occ: 2 (over core).
Axes of the slice: x: 2, y: 2, z: 4, core: 2. Of those that a mesh axis runs over, the one named last changes fastest.
Arguments:
- trial_singles: bfloat16 [8, 96], P('root'), may hold values from -6 to 6
- trial_doubles: bfloat16 [8, 480, 9216], P('root', 'virt', 'occ'), may hold values from -6 to 6
- occ_fock: bfloat16 [96, 96], replicated, may hold values from -0.625 to 0.625
- virt_fock: bfloat16 [480, 480], replicated, may hold values from -0.25 to 0.25
- w_ovoo: bfloat16 [96, 480, 9216], P('occ', 'virt', 'root'), may hold values from -0.625 to 0.625
- w_ooov: bfloat16 [96, 480, 9216], P('occ', 'virt', 'root'), may hold values from -0.0029296875 to 0.0029296875
- converged: int32 [8], replicated, may hold values from 0 to 1, as said below
Outputs:
- sigma_doubles: bfloat16 [8, 480, 9216], P('root', 'virt', 'occ')
- sigma_singles: float32 [8, 96], P('root')
- subspace: float32 [8, 8], P('root')
Inputs may be any that keep to these rules, and one draw needn't show every extreme that they name: `converged`: exactly 4 roots are active (0). In every draw at least one aligned block of 2 roots has all its roots active; other blocks may have none.
All inputs are finite; a program needn't handle non-finite values.
Results may differ from a plain program's by a relative error of at most 0.0044.
Values may be sent and summed in bfloat16 or wider, within the bound.
A program may use at most 256 MiB of HBM per device.

v0:
```python
import math
import jax
import jax.numpy as jnp
from jax import lax
from jax.sharding import PartitionSpec as P


def flat_pairs(left, right):
    return lax.dot_general(
        left.reshape(left.shape[0], -1),
        right.reshape(right.shape[0], -1),
        (((1,), (1,)), ((), ())),
        preferred_element_type=jnp.float32,
    )


def local(trial_singles, trial_doubles, occ_fock, virt_fock, w_ovoo, w_ooov, converged):
    local_roots, virt_local, pair_local = trial_doubles.shape
    occ_count = occ_fock.shape[0]
    virt_count = virt_fock.shape[0]
    root_count = converged.shape[0]
    root_groups = lax.axis_size("root")
    occ_groups = lax.axis_size("occ")
    root_index = lax.axis_index("root")
    occ_index = lax.axis_index("occ")
    occ_half = occ_count // occ_groups
    block_pairs = occ_count * occ_count // root_groups
    own_start = occ_index * occ_half
    active = (1 - converged).astype(jnp.float32)
    own_active = lax.dynamic_slice_in_dim(active, root_index * local_roots, local_roots)
    singles_all = lax.all_gather(trial_singles, "root", axis=0, tiled=True)
    gathered = lax.all_gather(trial_doubles, "occ", axis=2, tiled=True)
    fock_cols = lax.dynamic_slice_in_dim(occ_fock, own_start, occ_half, 1)
    batch_rows = local_roots * virt_local
    stacked = gathered.reshape(batch_rows, occ_count, occ_count)
    first_term = jnp.einsum(
        "ki,bkj->bij", fock_cols, stacked, preferred_element_type=jnp.float32
    ).reshape(local_roots, virt_local, pair_local)
    own_rows = trial_doubles.reshape(batch_rows, occ_half, occ_count)
    second_term = jnp.einsum(
        "bik,kj->bij", own_rows, occ_fock, preferred_element_type=jnp.float32
    ).reshape(local_roots, virt_local, pair_local)
    doubles_block = lax.all_to_all(gathered, "root", split_axis=2, concat_axis=0, tiled=True)
    partial_coupling = flat_pairs(doubles_block, w_ooov)
    coupling_part = lax.dynamic_update_slice(
        jnp.zeros((root_count, occ_count), jnp.float32), partial_coupling, (jnp.int32(0), own_start)
    )
    coupling = lax.psum(coupling_part, ("root", "virt", "occ"))
    singles_fock = jnp.dot(singles_all, occ_fock, preferred_element_type=jnp.float32)
    singles_every = active[:, None] * (-singles_fock - 0.5 * coupling)
    sigma_singles = lax.dynamic_slice_in_dim(singles_every, root_index * local_roots, local_roots)
    singles_cols = lax.dynamic_slice_in_dim(singles_all, own_start, occ_half, 1)
    outer_part = (
        -jnp.dot(singles_cols, w_ovoo.reshape(occ_half, -1), preferred_element_type=jnp.float32)
    ).reshape(root_count, virt_local, block_pairs)
    product = jnp.einsum(
        "ac,ncp->nap",
        virt_fock,
        lax.all_to_all(trial_doubles, "virt", split_axis=2, concat_axis=1, tiled=True),
        preferred_element_type=jnp.float32,
    ).astype(jnp.bfloat16)
    vv_term = lax.all_to_all(product, "virt", split_axis=1, concat_axis=2, tiled=True)
    vv_value = vv_term.astype(jnp.float32)
    outer_own = lax.all_to_all(outer_part, "root", split_axis=0, concat_axis=2, tiled=True)
    outer_half = lax.psum_scatter(outer_own, "occ", scatter_dimension=2, tiled=True)
    summed = vv_value + outer_half - first_term - second_term
    sigma_doubles = (own_active[:, None, None] * summed).astype(jnp.bfloat16)
    trial_piece, sigma_piece = (
        lax.all_to_all(trial_doubles, "root", split_axis=2, concat_axis=0, tiled=True),
        lax.all_to_all(sigma_doubles, "root", split_axis=2, concat_axis=0, tiled=True),
    )
    doubles_part = lax.psum(flat_pairs(trial_piece, sigma_piece), ("root", "virt", "occ"))
    singles_part = jnp.dot(
        singles_all.astype(jnp.float32), singles_every.T, precision=lax.Precision.HIGHEST
    )
    whole_matrix = doubles_part / math.sqrt(
        occ_count * occ_count * virt_count
    ) + singles_part / math.sqrt(occ_count)
    subspace = lax.dynamic_slice_in_dim(whole_matrix, root_index * local_roots, local_roots, 0)
    return (sigma_doubles, sigma_singles, subspace)


def solution(mesh):
    placed = (
        P("root", None),
        P("root", "virt", "occ"),
        P(),
        P(),
        P("occ", "virt", "root"),
        P("occ", "virt", "root"),
        P(),
    )
    return jax.shard_map(
        local,
        mesh=mesh,
        in_specs=placed,
        out_specs=(P("root", "virt", "occ"), P("root", None), P("root", None)),
        check_vma=False,
    )
```

profile of v0, /device:TPU:0, one launch (start us, length us, event | category | flops | bytes accessed | tf_op | source)
XLA Modules:
  0.0 595.7 jit_solution(10986336026013833331)
XLA Ops:
  7.2 6.9 %copy.53 = bf16[2,120,4608]{1,0,2:T(2,128)(2,1)} copy(bf16[2,120,4608]{2,1,0:T(8,128)(2,1)} %param.8) | data formatting | bytes 4423680 | tf_op args[1]
  14.1 5.2 all-to-all-start
  19.3 24.4 %copy.79 = bf16[6,8,120,2304]{3,1,2,0:T(8,128)(2,1)} copy(bf16[6,8,120,2304]{3,2,1,0:T(8,128)(2,1)} %bitcast.88) | data formatting | bytes 53084160
  43.7 11.1 %all-gather = bf16[4,2,96]{2,1,0:T(2,128)(2,1)S(1)} all-gather(bf16[1,2,96]{2,1,0:T(2,128)(2,1)S(1)} %bitcast.102), channel_id=1, replica_groups=mesh['root'=4,'virt'=4,'occ'=2] {'root'}, dimensions={0}, use_global_device_ids=true | all-gather | bytes 1920 | tf_op jit(solution)/shard_map/all_gather | solution.py:31
  54.8 10.4 %convolution_negate_fusion = f32[8,276480]{1,0:T(8,128)S(1)} fusion(bf16[48,276480]{1,0:T(8,128)(2,1)} %bitcast.84, bf16[8,96]{1,0:T(8,128)(2,1)S(1)} %bitcast.99, s32[]{:T(128)S(6)} %select_n.5), kind=kOutput, calls=%fused_computation | convolution fusion | flops 214548480 | bytes 35390980 | tf_op jit(solution)/shard_map/dot_general | solution.py:54
  65.3 6.1 %copy.57 = f32[8,120,2304]{2,1,0:T(8,128)} copy(f32[8,120,2304]{2,0,1:T(8,128)S(1)} %bitcast.85) | data formatting | bytes 17694720 | tf_op jit(solution)/shard_map/reshape | solution.py:55
  71.4 5.7 all-to-all-start.2
  77.8 4.4 copy.54
  88.3 180.0 %all-to-all-done.2 = f32[8,120,2304]{2,1,0:T(8,128)} async-done(((f32[8,120,2304]{2,1,0:T(8,128)}), f32[8,120,2304]{2,1,0:T(8,128)}, u32[]{:S(2)}, u32[]{:S(2)}) %all-to-all-start.2) | async-done | bytes 8847392 | tf_op jit(solution)/shard_map/all_to_all | solution.py:64
  272.1 14.5 %copy.58 = f32[2,120,4,2304]{1,0,3,2:T(2,128)} copy(f32[2,120,4,2304]{3,1,0,2:T(8,128)} %bitcast.12) | data formatting | bytes 17694720 | tf_op jit(solution)/shard_map/all_to_all | solution.py:64
  286.6 10.8 %all-to-all-done.1 = bf16[2,480,1152]{2,0,1:T(2,128)(2,1)S(1)} async-done(((bf16[2,480,1152]{2,0,1:T(2,128)(2,1)}), bf16[2,480,1152]{2,0,1:T(2,128)(2,1)S(1)}, u32[]{:S(2)}, u32[]{:S(2)}) %all-to-all-start.1) | async-done | bytes 2211872 | tf_op jit(solution)/shard_map/all_to_all | solution.py:62
  302.6 12.7 %copy.65 = bf16[2,120,9216]{1,0,2:T(2,128)(2,1)} copy(bf16[2,120,9216]{2,1,0:T(8,128)(2,1)} %all-gather.3.cloned.1.call-done) | data formatting | bytes 8847360 | tf_op jit(solution)/shard_map/all_gather | solution.py:32
  315.3 40.6 %all-to-all-done.5 = bf16[2,120,4608]{1,0,2:T(2,128)(2,1)S(1)} async-done(((bf16[2,120,4608]{1,0,2:T(2,128)(2,1)}), bf16[2,120,4608]{1,0,2:T(2,128)(2,1)S(1)}, u32[]{:S(2)}, u32[]{:S(2)}) %all-to-all-start.5) | async-done | bytes 2211872 | tf_op jit(solution)/shard_map/all_to_all | solution.py:69
  356.0 5.1 all-to-all-start.3
  361.1 5.9 reshape.49
  367.0 4.7 fusion.11
  371.6 7.1 %reshape.50 = f32[2,120,4608]{1,0,2:T(2,128)} reshape(f32[240,48,96]{0,2,1:T(8,128)} %fusion.11) | data formatting | bytes 8847360 | tf_op jit(solution)/shard_map/reshape | solution.py:42
  380.1 8.9 %copy.56 = f32[2,4,120,1152]{2,0,3,1:T(2,128)} copy(bf16[2,4,120,1152]{3,0,2,1:T(2,128)(2,1)} %bitcast.95) | data formatting | bytes 6635520 | tf_op jit(solution)/shard_map/convert_element_type | solution.py:63
  389.0 9.5 %reshape.62 = bf16[240,96,96]{2,1,0:T(8,128)(2,1)} reshape(bf16[2,120,9216]{2,1,0:T(8,128)(2,1)} %all-gather.3.cloned.1.call-done) | data formatting | bytes 8847360 | tf_op jit(solution)/shard_map/reshape | solution.py:35
  398.6 9.2 %copy.61 = bf16[240,96,96]{0,1,2:T(8,128)(2,1)} copy(bf16[240,96,96]{2,1,0:T(8,128)(2,1)} %reshape.62) | data formatting | bytes 8847360 | tf_op jit(solution)/shard_map/reshape | solution.py:35
  411.0 4.8 copy.62
  415.9 7.1 %reshape.48 = f32[2,120,4608]{1,0,2:T(2,128)} reshape(f32[240,48,96]{0,2,1:T(8,128)} %copy.62) | data formatting | bytes 8847360 | tf_op jit(solution)/shard_map/reshape | solution.py:38
  423.0 10.2 %fusion.3 = bf16[2,120,4608]{1,0,2:T(2,128)(2,1)} fusion(f32[2,120,4608]{1,0,2:T(2,128)} %reshape.50, f32[2,120,4608]{1,0,2:T(2,128)} %reshape.48, f32[2,120,9216]{1,0,2:T(2,128)} %all-reduce.4.cloned.1.call-done, u32[]{:T(128)S(6)} %multiply.4, f32[2,4,120,1152]{2,0,3,1:T(2,128)} %copy.56, f32[2]{0:T(128)S(1)} %dynamic_slice.15), kind=kLoop, calls=%fused_computation.5 | loop fusion | flops 5529600 | bytes 19906572 | tf_op jit(solution)/shard_map/convert_element_type | solution.py:67
  433.2 31.7 %all-to-all-done.3 = bf16[2,120,9216]{1,0,2:T(2,128)(2,1)} async-done(((bf16[2,120,9216]{1,0,2:T(2,128)(2,1)}), bf16[2,120,9216]{1,0,2:T(2,128)(2,1)}, u32[]{:S(2)}, u32[]{:S(2)}) %all-to-all-start.3) | async-done | bytes 4423712 | tf_op jit(solution)/shard_map/all_to_all | solution.py:43
  464.9 4.7 all-to-all-start.4
  469.6 24.4 %copy.81 = bf16[6,8,120,2304]{3,1,2,0:T(8,128)(2,1)} copy(bf16[6,8,120,2304]{3,2,1,0:T(8,128)(2,1)} %bitcast.89) | data formatting | bytes 53084160
  500.2 12.3 %copy.66 = bf16[2,120,4,2304]{3,1,0,2:T(8,128)(2,1)} copy(bf16[2,120,4,2304]{1,0,3,2:T(2,128)(2,1)} %bitcast.17) | data formatting | bytes 8847360 | tf_op jit(solution)/shard_map/all_to_all | solution.py:43
  512.5 5.2 copy.80
  517.7 13.4 %fusion.17 = f32[8,48]{1,0:T(8,128)S(1)} fusion(bf16[8,276480]{1,0:T(8,128)(2,1)} %bitcast.87, bf16[48,276480]{1,0:T(8,128)(2,1)} %bitcast.83), kind=kOutput, calls=%fused_computation.27 | convolution fusion | flops 212336640 | bytes 30967296 | tf_op jit(solution)/shard_map/dot_general | solution.py:9
  531.2 6.7 %copy.71 = bf16[2,120,4608]{2,1,0:T(8,128)(2,1)} copy(bf16[2,120,4608]{1,0,2:T(2,128)(2,1)} %fusion.3) | data formatting | bytes 4423680
  537.9 6.8 %copy.67 = bf16[2,120,4,1152]{3,1,0,2:T(8,128)(2,1)} copy(bf16[2,120,4,1152]{1,0,3,2:T(2,128)(2,1)} %bitcast.19) | data formatting | bytes 4423680 | tf_op jit(solution)/shard_map/all_to_all | solution.py:70
  547.8 39.5 %all-reduce.1 = (f32[8,96]{1,0:T(8,128)S(1)}, f32[8,8]{0,1:T(8,128)S(1)}) all-reduce(f32[8,96]{1,0:T(8,128)S(1)} %dynamic_update_slice.3, f32[8,8]{0,1:T(8,128)S(1)} %convolution_bitcast_fusion.1), channel_id=1, replica_groups=mesh['root'=4,'virt'=4,'occ'=2] {'root','virt','occ'}, use_global_device_ids=true, to_apply=%region_1.0 | all-reduce | flops 832 | bytes 6656 | tf_op jit(solution)/shard_map/psum | solution.py:48
  (41 shorter events, 30.6 us)
Async XLA Ops:
  7.2 75.1 %copy-start = (bf16[480,480]{1,0:T(8,128)(2,1)S(1)}, bf16[480,480]{1,0:T(8,128)(2,1)}, u32[]{:S(2)}) copy-start(bf16[480,480]{1,0:T(8,128)(2,1)} %param.10) | copy-start | bytes 1382404
  14.1 57.3 %all-to-all-start = ((bf16[2,120,4608]{1,0,2:T(2,128)(2,1)}), bf16[2,120,4608]{1,0,2:T(2,128)(2,1)S(1)}, u32[]{:S(2)}, u32[]{:S(2)}) async-start(bf16[2,120,4608]{1,0,2:T(2,128)(2,1)} %copy.53), calls=%async_computation | async-start | bytes 4718592 | tf_op jit(solution)/shard_map/all_to_all | solution.py:59
  19.3 24.4 %copy-start.4 = (bf16[2,96]{1,0:T(2,128)(2,1)S(1)}, bf16[2,96]{1,0:T(2,128)(2,1)}, u32[]{:S(2)}) copy-start(bf16[2,96]{1,0:T(2,128)(2,1)} %param.7) | copy-start | bytes 1156
  71.4 196.8 %all-to-all-start.2 = ((f32[8,120,2304]{2,1,0:T(8,128)}), f32[8,120,2304]{2,1,0:T(8,128)}, u32[]{:S(2)}, u32[]{:S(2)}) async-start(f32[8,120,2304]{2,1,0:T(8,128)} %copy.57), calls=%async_computation.2 | async-start | bytes 17694720 | tf_op jit(solution)/shard_map/all_to_all | solution.py:64
  77.1 225.4 %all-gather.3.cloned.1.call-start = ((), (), s32[]{:S(2)}) async-start(), calls=%async_computation.6 | async-start | bytes 6635520 | tf_op jit(solution)/shard_map/all_gather | solution.py:32
  268.2 29.2 %all-to-all-start.1 = ((bf16[2,480,1152]{2,0,1:T(2,128)(2,1)}), bf16[2,480,1152]{2,0,1:T(2,128)(2,1)S(1)}, u32[]{:S(2)}, u32[]{:S(2)}) async-start(bf16[2,480,1152]{2,0,1:T(2,128)(2,1)} %copy.55), calls=%async_computation.1 | async-start | bytes 4423680 | tf_op jit(solution)/shard_map/all_to_all | solution.py:62
  272.1 150.9 %all-reduce.4.cloned.1.call-start = ((), (), s32[]{:S(2)}) async-start(), calls=%async_computation.7 | async-start | bytes 18874368
  297.5 1.4 copy-start.2
  298.8 57.1 %all-to-all-start.5 = ((bf16[2,120,4608]{1,0,2:T(2,128)(2,1)}), bf16[2,120,4608]{1,0,2:T(2,128)(2,1)S(1)}, u32[]{:S(2)}, u32[]{:S(2)}) async-start(bf16[2,120,4608]{1,0,2:T(2,128)(2,1)} %copy.53), calls=%async_computation.5 | async-start | bytes 4718592 | tf_op jit(solution)/shard_map/all_to_all | solution.py:69
  356.0 108.9 %all-to-all-start.3 = ((bf16[2,120,9216]{1,0,2:T(2,128)(2,1)}), bf16[2,120,9216]{1,0,2:T(2,128)(2,1)}, u32[]{:S(2)}, u32[]{:S(2)}) async-start(bf16[2,120,9216]{1,0,2:T(2,128)(2,1)} %copy.65), calls=%async_computation.3 | async-start | bytes 9437184 | tf_op jit(solution)/shard_map/all_to_all | solution.py:43
  361.1 5.9 copy-start.3
  371.6 7.2 %copy-start.5 = (s32[8]{0:T(128)S(1)}, s32[8]{0:T(128)}, u32[]{:S(2)}) copy-start(s32[8]{0:T(128)} %param.13) | copy-start | bytes 100
  371.6 7.2 %copy-start.6 = (u32[32]{0:T(128)S(1)}, u32[32]{0:T(128)}, u32[]{:S(2)}) copy-start(u32[32]{0:T(128)} %constant.35) | copy-start | bytes 388
  464.9 73.0 %all-to-all-start.4 = ((bf16[2,120,4608]{1,0,2:T(2,128)(2,1)}), bf16[2,120,4608]{1,0,2:T(2,128)(2,1)}, u32[]{:S(2)}, u32[]{:S(2)}) async-start(bf16[2,120,4608]{1,0,2:T(2,128)(2,1)} %fusion.3), calls=%async_computation.4 | async-start | bytes 4718592 | tf_op jit(solution)/shard_map/all_to_all | solution.py:70
  537.9 51.0 %copy-start.1 = (bf16[480,480]{1,0:T(8,128)(2,1)S(1)}, bf16[480,480]{1,0:T(8,128)(2,1)}, u32[]{:S(2)}) copy-start(bf16[480,480]{1,0:T(8,128)(2,1)} %param.10) | copy-start | bytes 1382404
Sparse Core Ops, SparseCore 0:
  79.5 15.8 all-gather.2
  286.7 40.7 all-reduce.3
where the time goes:
time: 599 us; the launch traced here: 596 us
  waiting for transfers between devices  264 us (44%)
  local copies, waits for them, and re-layouts  192 us (32%)
  blocking collectives  50.7 us (8%)
  matrix products  36.1 us (6%)
  starting transfers between devices  28.3 us (5%)
  between operations  14.8 us (2%)
  other arithmetic  10.2 us (2%)
    all_to_all x1, waiting for transfers between devices, local(): lax.all_to_all(outer_part, 'root', split_axis=0, concat_axis=2, tiled=True)  180 us
    unnamed x23, local copies, waits for them, and re-layouts  74 us
    all_to_all x1, waiting for transfers between devices, local(): lax.all_to_all(trial_doubles, 'root', split_axis=2, concat_axis=0, tiled=...  40.6 us
    psum x1, blocking collectives, local(): coupling = lax.psum(coupling_part, ('root', 'virt', 'occ'))  39.5 us
    all_to_all x1, waiting for transfers between devices, local(): lax.all_to_all(gathered, 'root', split_axis=2, concat_axis=0, tiled=True)  31.7 us
    reshape x2, local copies, waits for them, and re-layouts, local(): stacked = gathered.reshape(batch_rows, occ_count, occ_count)  18.8 us
    dot_general x2, matrix products, flat_pairs(): lax.dot_general(left.reshape(left.shape[0], -1), right.reshape(right.shap...  14.6 us
    all_to_all x1, local copies, waits for them, and re-layouts, local(): lax.all_to_all(outer_part, 'root', split_axis=0, concat_axis=2, tiled=True)  14.5 us
  transfers between devices with their start and end apart: 8, of which 4 were waited for; matrix products, arithmetic and copies ran while one was open for 37% of the time, Pallas kernels for 0%

commit v1 on v0

--- a/solution.py
+++ b/solution.py
@@ -45,7 +45,7 @@
     coupling_part = lax.dynamic_update_slice(
         jnp.zeros((root_count, occ_count), jnp.float32), partial_coupling, (jnp.int32(0), own_start)
     )
-    coupling = lax.psum(coupling_part, ("root", "virt", "occ"))
+    coupling = jnp.sum(lax.all_gather(coupling_part, ("root", "virt", "occ")), axis=0)
     singles_fock = jnp.dot(singles_all, occ_fock, preferred_element_type=jnp.float32)
     singles_every = active[:, None] * (-singles_fock - 0.5 * coupling)
     sigma_singles = lax.dynamic_slice_in_dim(singles_every, root_index * local_roots, local_roots)

time: 599 us -> 637 us (1.063)
  blocking collectives: 50.7 us -> 87.8 us
    all_gather x0 -> x1, blocking collectives: none -> 39.8 us  [local(): lax.all_gather(coupling_part, ('root', 'virt', 'occ'))]
  transfers between devices with their start and end apart: 8 -> 8, of which waited for: 4 -> 4; matrix products, arithmetic and copies ran while one was open for 37% -> 35% of each run, Pallas kernels for 0% -> 0%
where the time goes in v1:
time: 637 us; the launch traced here: 633 us
  waiting for transfers between devices  264 us (41%)
  local copies, waits for them, and re-layouts  192 us (30%)
  blocking collectives  87.8 us (14%)
  matrix products  36.1 us (6%)
  starting transfers between devices  28.4 us (4%)
  between operations  14.8 us (2%)
  other arithmetic  10.2 us (2%)
    all_to_all x1, waiting for transfers between devices, local(): lax.all_to_all(outer_part, 'root', split_axis=0, concat_axis=2, tiled=True)  180 us
    unnamed x23, local copies, waits for them, and re-layouts  74 us
    all_to_all x1, waiting for transfers between devices, local(): lax.all_to_all(trial_doubles, 'root', split_axis=2, concat_axis=0, tiled=...  40.7 us
    all_gather x1, blocking collectives, local(): lax.all_gather(coupling_part, ('root', 'virt', 'occ'))  39.8 us
    psum x1, blocking collectives, local(): lax.psum(flat_pairs(trial_piece, sigma_piece), ('root', 'virt', 'occ'))  36.8 us
    all_to_all x1, waiting for transfers between devices, local(): lax.all_to_all(gathered, 'root', split_axis=2, concat_axis=0, tiled=True)  31.6 us
    reshape x2, local copies, waits for them, and re-layouts, local(): stacked = gathered.reshape(batch_rows, occ_count, occ_count)  18.8 us
    dot_general x2, matrix products, flat_pairs(): lax.dot_general(left.reshape(left.shape[0], -1), right.reshape(right.shap...  14.6 us
  transfers between devices with their start and end apart: 8, of which 4 were waited for; matrix products, arithmetic and copies ran while one was open for 35% of the time, Pallas kernels for 0%

profile of v1, /device:TPU:0, one launch (start us, length us, event | category | flops | bytes accessed | tf_op | source)
XLA Modules:
  0.0 633.0 jit_solution(2538199939010365140)
XLA Ops:
  7.2 6.9 %copy.53 = bf16[2,120,4608]{1,0,2:T(2,128)(2,1)} copy(bf16[2,120,4608]{2,1,0:T(8,128)(2,1)} %param.8) | data formatting | bytes 4423680 | tf_op args[1]
  14.1 5.2 all-to-all-start
  19.3 24.4 %copy.79 = bf16[6,8,120,2304]{3,1,2,0:T(8,128)(2,1)} copy(bf16[6,8,120,2304]{3,2,1,0:T(8,128)(2,1)} %bitcast.90) | data formatting | bytes 53084160
  43.7 11.1 %all-gather = bf16[4,2,96]{2,1,0:T(2,128)(2,1)S(1)} all-gather(bf16[1,2,96]{2,1,0:T(2,128)(2,1)S(1)} %bitcast.104), channel_id=1, replica_groups=mesh['root'=4,'virt'=4,'occ'=2] {'root'}, dimensions={0}, use_global_device_ids=true | all-gather | bytes 1920 | tf_op jit(solution)/shard_map/all_gather | solution.py:31
  54.8 10.4 %convolution_negate_fusion = f32[8,276480]{1,0:T(8,128)S(1)} fusion(bf16[48,276480]{1,0:T(8,128)(2,1)} %bitcast.86, bf16[8,96]{1,0:T(8,128)(2,1)S(1)} %bitcast.101, s32[]{:T(128)S(6)} %select_n.5), kind=kOutput, calls=%fused_computation | convolution fusion | flops 214548480 | bytes 35390980 | tf_op jit(solution)/shard_map/dot_general | solution.py:54
  65.3 6.1 copy.57
  71.4 5.7 all-to-all-start.2
  88.3 180.0 %all-to-all-done.2 = f32[8,120,2304]{2,1,0:T(8,128)} async-done(((f32[8,120,2304]{2,1,0:T(8,128)}), f32[8,120,2304]{2,1,0:T(8,128)}, u32[]{:S(2)}, u32[]{:S(2)}) %all-to-all-start.2) | async-done | bytes 8847392 | tf_op jit(solution)/shard_map/all_to_all | solution.py:64
  272.1 14.6 %copy.58 = f32[2,120,4,2304]{1,0,3,2:T(2,128)} copy(f32[2,120,4,2304]{3,1,0,2:T(8,128)} %bitcast.12) | data formatting | bytes 17694720 | tf_op jit(solution)/shard_map/all_to_all | solution.py:64
  286.7 10.8 %all-to-all-done.1 = bf16[2,480,1152]{2,0,1:T(2,128)(2,1)S(1)} async-done(((bf16[2,480,1152]{2,0,1:T(2,128)(2,1)}), bf16[2,480,1152]{2,0,1:T(2,128)(2,1)S(1)}, u32[]{:S(2)}, u32[]{:S(2)}) %all-to-all-start.1) | async-done | bytes 2211872 | tf_op jit(solution)/shard_map/all_to_all | solution.py:62
  302.6 12.7 %copy.65 = bf16[2,120,9216]{1,0,2:T(2,128)(2,1)} copy(bf16[2,120,9216]{2,1,0:T(8,128)(2,1)} %all-gather.3.cloned.1.call-done) | data formatting | bytes 8847360 | tf_op jit(solution)/shard_map/all_gather | solution.py:32
  315.3 40.7 %all-to-all-done.5 = bf16[2,120,4608]{1,0,2:T(2,128)(2,1)S(1)} async-done(((bf16[2,120,4608]{1,0,2:T(2,128)(2,1)}), bf16[2,120,4608]{1,0,2:T(2,128)(2,1)S(1)}, u32[]{:S(2)}, u32[]{:S(2)}) %all-to-all-start.5) | async-done | bytes 2211872 | tf_op jit(solution)/shard_map/all_to_all | solution.py:69
  356.0 5.1 all-to-all-start.3
  361.1 5.9 reshape.51
  367.0 4.7 fusion.11
  371.7 7.2 %reshape.52 = f32[2,120,4608]{1,0,2:T(2,128)} reshape(f32[240,48,96]{0,2,1:T(8,128)} %fusion.11) | data formatting | bytes 8847360 | tf_op jit(solution)/shard_map/reshape | solution.py:42
  380.2 8.9 %copy.56 = f32[2,4,120,1152]{2,0,3,1:T(2,128)} copy(bf16[2,4,120,1152]{3,0,2,1:T(2,128)(2,1)} %bitcast.97) | data formatting | bytes 6635520 | tf_op jit(solution)/shard_map/convert_element_type | solution.py:63
  389.1 9.5 %reshape.64 = bf16[240,96,96]{2,1,0:T(8,128)(2,1)} reshape(bf16[2,120,9216]{2,1,0:T(8,128)(2,1)} %all-gather.3.cloned.1.call-done) | data formatting | bytes 8847360 | tf_op jit(solution)/shard_map/reshape | solution.py:35
  398.7 9.2 %copy.61 = bf16[240,96,96]{0,1,2:T(8,128)(2,1)} copy(bf16[240,96,96]{2,1,0:T(8,128)(2,1)} %reshape.64) | data formatting | bytes 8847360 | tf_op jit(solution)/shard_map/reshape | solution.py:35
  411.1 4.8 copy.62
  416.0 7.1 %reshape.50 = f32[2,120,4608]{1,0,2:T(2,128)} reshape(f32[240,48,96]{0,2,1:T(8,128)} %copy.62) | data formatting | bytes 8847360 | tf_op jit(solution)/shard_map/reshape | solution.py:38
  423.1 10.2 %fusion.3 = bf16[2,120,4608]{1,0,2:T(2,128)(2,1)} fusion(f32[2,120,4608]{1,0,2:T(2,128)} %reshape.52, f32[2,120,4608]{1,0,2:T(2,128)} %reshape.50, f32[2,120,9216]{1,0,2:T(2,128)} %all-reduce.3.cloned.1.call-done, u32[]{:T(128)S(6)} %multiply.4, f32[2,4,120,1152]{2,0,3,1:T(2,128)} %copy.56, f32[2]{0:T(128)S(1)} %dynamic_slice.15), kind=kLoop, calls=%fused_computation.5 | loop fusion | flops 5529600 | bytes 19906572 | tf_op jit(solution)/shard_map/convert_element_type | solution.py:67
  433.3 31.6 %all-to-all-done.3 = bf16[2,120,9216]{1,0,2:T(2,128)(2,1)} async-done(((bf16[2,120,9216]{1,0,2:T(2,128)(2,1)}), bf16[2,120,9216]{1,0,2:T(2,128)(2,1)}, u32[]{:S(2)}, u32[]{:S(2)}) %all-to-all-start.3) | async-done | bytes 4423712 | tf_op jit(solution)/shard_map/all_to_all | solution.py:43
  464.9 4.7 all-to-all-start.4
  469.7 24.4 %copy.81 = bf16[6,8,120,2304]{3,1,2,0:T(8,128)(2,1)} copy(bf16[6,8,120,2304]{3,2,1,0:T(8,128)(2,1)} %bitcast.91) | data formatting | bytes 53084160
  500.3 12.3 %copy.66 = bf16[2,120,4,2304]{3,1,0,2:T(8,128)(2,1)} copy(bf16[2,120,4,2304]{1,0,3,2:T(2,128)(2,1)} %bitcast.17) | data formatting | bytes 8847360 | tf_op jit(solution)/shard_map/all_to_all | solution.py:43
  512.6 5.2 copy.80
  517.8 13.4 %convolution_bitcast_fusion.1 = f32[1,8,48]{2,1,0:T(8,128)S(1)} fusion(bf16[8,276480]{1,0:T(8,128)(2,1)} %bitcast.89, bf16[48,276480]{1,0:T(8,128)(2,1)} %bitcast.85), kind=kOutput, calls=%fused_computation.12 | convolution fusion | flops 212336640 | bytes 30967296 | tf_op jit(solution)/shard_map/dot_general | solution.py:9
  531.3 39.8 %all_gather.15 = f32[32,8,96]{2,1,0:T(8,128)S(1)} all-gather(f32[1,8,96]{2,1,0:T(8,128)S(1)} %dynamic_update_slice.4), channel_id=1, replica_groups=mesh['root'=4,'virt'=4,'occ'=2] {'root','virt','occ'}, dimensions={0}, use_global_device_ids=true | all-gather | bytes 101376 | tf_op jit(solution)/shard_map/all_gather | solution.py:48
  571.9 6.7 %copy.71 = bf16[2,120,4608]{2,1,0:T(8,128)(2,1)} copy(bf16[2,120,4608]{1,0,2:T(2,128)(2,1)} %fusion.3) | data formatting | bytes 4423680
  578.6 6.8 %copy.67 = bf16[2,120,4,1152]{3,1,0,2:T(8,128)(2,1)} copy(bf16[2,120,4,1152]{1,0,3,2:T(2,128)(2,1)} %bitcast.20) | data formatting | bytes 4423680 | tf_op jit(solution)/shard_map/all_to_all | solution.py:70
  588.5 36.8 %psum.7 = f32[8,8]{0,1:T(8,128)S(1)} all-reduce(f32[8,8]{0,1:T(8,128)S(1)} %convolution_bitcast_fusion.2), channel_id=1, replica_groups=mesh['root'=4,'virt'=4,'occ'=2] {'root','virt','occ'}, use_global_device_ids=true, to_apply=%region_2.0 | all-reduce | flops 64 | bytes 512 | tf_op jit(solution)/shard_map/psum | solution.py:72
  (43 shorter events, 35.0 us)
Async XLA Ops:
  7.2 75.1 %copy-start = (bf16[480,480]{1,0:T(8,128)(2,1)S(1)}, bf16[480,480]{1,0:T(8,128)(2,1)}, u32[]{:S(2)}) copy-start(bf16[480,480]{1,0:T(8,128)(2,1)} %param.10) | copy-start | bytes 1382404
  14.1 57.4 %all-to-all-start = ((bf16[2,120,4608]{1,0,2:T(2,128)(2,1)}), bf16[2,120,4608]{1,0,2:T(2,128)(2,1)S(1)}, u32[]{:S(2)}, u32[]{:S(2)}) async-start(bf16[2,120,4608]{1,0,2:T(2,128)(2,1)} %copy.53), calls=%async_computation | async-start | bytes 4718592 | tf_op jit(solution)/shard_map/all_to_all | solution.py:59
  19.3 24.4 %copy-start.4 = (bf16[2,96]{1,0:T(2,128)(2,1)S(1)}, bf16[2,96]{1,0:T(2,128)(2,1)}, u32[]{:S(2)}) copy-start(bf16[2,96]{1,0:T(2,128)(2,1)} %param.7) | copy-start | bytes 1156
  71.4 196.8 %all-to-all-start.2 = ((f32[8,120,2304]{2,1,0:T(8,128)}), f32[8,120,2304]{2,1,0:T(8,128)}, u32[]{:S(2)}, u32[]{:S(2)}) async-start(f32[8,120,2304]{2,1,0:T(8,128)} %copy.57), calls=%async_computation.2 | async-start | bytes 17694720 | tf_op jit(solution)/shard_map/all_to_all | solution.py:64
  77.1 225.4 %all-gather.3.cloned.1.call-start = ((), (), s32[]{:S(2)}) async-start(), calls=%async_computation.6 | async-start | bytes 6635520 | tf_op jit(solution)/shard_map/all_gather | solution.py:32
  268.2 29.2 %all-to-all-start.1 = ((bf16[2,480,1152]{2,0,1:T(2,128)(2,1)}), bf16[2,480,1152]{2,0,1:T(2,128)(2,1)S(1)}, u32[]{:S(2)}, u32[]{:S(2)}) async-start(bf16[2,480,1152]{2,0,1:T(2,128)(2,1)} %copy.55), calls=%async_computation.1 | async-start | bytes 4423680 | tf_op jit(solution)/shard_map/all_to_all | solution.py:62
  272.1 151.0 %all-reduce.3.cloned.1.call-start = ((), (), s32[]{:S(2)}) async-start(), calls=%async_computation.7 | async-start | bytes 18874368
  297.5 1.4 copy-start.2
  298.9 57.2 %all-to-all-start.5 = ((bf16[2,120,4608]{1,0,2:T(2,128)(2,1)}), bf16[2,120,4608]{1,0,2:T(2,128)(2,1)S(1)}, u32[]{:S(2)}, u32[]{:S(2)}) async-start(bf16[2,120,4608]{1,0,2:T(2,128)(2,1)} %copy.53), calls=%async_computation.5 | async-start | bytes 4718592 | tf_op jit(solution)/shard_map/all_to_all | solution.py:69
  356.0 108.9 %all-to-all-start.3 = ((bf16[2,120,9216]{1,0,2:T(2,128)(2,1)}), bf16[2,120,9216]{1,0,2:T(2,128)(2,1)}, u32[]{:S(2)}, u32[]{:S(2)}) async-start(bf16[2,120,9216]{1,0,2:T(2,128)(2,1)} %copy.65), calls=%async_computation.3 | async-start | bytes 9437184 | tf_op jit(solution)/shard_map/all_to_all | solution.py:43
  361.1 5.9 copy-start.3
  371.7 7.2 %copy-start.5 = (s32[8]{0:T(128)S(1)}, s32[8]{0:T(128)}, u32[]{:S(2)}) copy-start(s32[8]{0:T(128)} %param.13) | copy-start | bytes 100
  371.7 7.3 %copy-start.6 = (u32[32]{0:T(128)S(1)}, u32[32]{0:T(128)}, u32[]{:S(2)}) copy-start(u32[32]{0:T(128)} %constant.37) | copy-start | bytes 388
  464.9 113.6 %all-to-all-start.4 = ((bf16[2,120,4608]{1,0,2:T(2,128)(2,1)}), bf16[2,120,4608]{1,0,2:T(2,128)(2,1)}, u32[]{:S(2)}, u32[]{:S(2)}) async-start(bf16[2,120,4608]{1,0,2:T(2,128)(2,1)} %fusion.3), calls=%async_computation.4 | async-start | bytes 4718592 | tf_op jit(solution)/shard_map/all_to_all | solution.py:70
  578.6 47.6 %copy-start.1 = (bf16[480,480]{1,0:T(8,128)(2,1)S(1)}, bf16[480,480]{1,0:T(8,128)(2,1)}, u32[]{:S(2)}) copy-start(bf16[480,480]{1,0:T(8,128)(2,1)} %param.10) | copy-start | bytes 1382404
Sparse Core Ops, SparseCore 0:
  79.5 15.8 all-gather.2
  286.8 40.7 all-reduce.2
